TPU v7x, 32 devices: a whole 2x2x4 slice. The times are simulated.
32 devices in a mesh: elem: 8 (over z, y), bucket: 4 (over x, core).
Axes of the slice: x: 2, y: 2, z: 4, core: 2. Of those that a mesh axis runs over, the one named last changes fastest.
Arguments:
- node_data: float32 [24, 98304], P(None, 'elem'), may hold values from -6 to 6
- eroded: int32 [4096], P('elem'), may hold values from 0 to 2047, as said below
- bucket_map: int32 [98304], P('elem'), may hold values from 0 to 63, as said below
- seg_point: float32 [64, 3, 512], P('elem', None, 'bucket'), may hold values from -3 to 3
- seg_angle: float32 [64, 2, 512], P('elem', None, 'bucket'), may hold values from -3.140625 to 3.140625
Outputs:
- face_force: float32 [3, 24576], P(None, 'elem')
Inputs may be any that keep to these rules, and one draw needn't show every extreme that they name: `eroded`: the 512 entries of one index of elem are distinct local element numbers. `bucket_map`: among the faces of the elements listed in eroded, those of one index of elem name one bucket at most 80 times; in every draw some bucket is named exactly 80 times by every index of elem.
All inputs are finite; a program needn't handle non-finite values.
Results may differ from a plain program's by a relative error of at most 0.00012.
Values sent between devices are 32-bit elements; how exact they have to be, the bound alone decides.
A program may use at most 64 MiB of HBM per device.

v0:
```python
import jax
import jax.numpy as jnp
from jax import lax
from jax.sharding import PartitionSpec as P

STIFFNESS = 20.0
DAMPING = 0.5


def face_geometry(payload):
    corner = payload[0:12].reshape(4, 3, -1)
    motion = payload[12:24].reshape(4, 3, -1)
    centroid = 0.25 * (corner[0] + corner[1] + corner[2] + corner[3])
    first_edge = corner[2] - corner[0]
    second_edge = corner[3] - corner[1]
    area_x = 0.5 * (first_edge[1] * second_edge[2] - first_edge[2] * second_edge[1])
    area_y = 0.5 * (first_edge[2] * second_edge[0] - first_edge[0] * second_edge[2])
    area_z = 0.5 * (first_edge[0] * second_edge[1] - first_edge[1] * second_edge[0])
    velocity = 0.25 * (motion[0] + motion[1] + motion[2] + motion[3])
    return jnp.concatenate([centroid, jnp.stack([area_x, area_y, area_z]), velocity], axis=0)


def unit_normal(angles):
    return jnp.stack(
        [
            jnp.cos(angles[:, 0]) * jnp.sin(angles[:, 1]),
            jnp.sin(angles[:, 0]) * jnp.sin(angles[:, 1]),
            jnp.cos(angles[:, 1]),
        ],
        axis=1,
    )


def penalty_terms(geometry, point, normal, stiff):
    offset = geometry[0:3, :, None] - point
    dist_sq = offset[0] * offset[0] + offset[1] * offset[1] + offset[2] * offset[2]
    gap_value = offset[0] * normal[0] + offset[1] * normal[1] + offset[2] * normal[2]
    closing = (
        geometry[6][:, None] * normal[0]
        + geometry[7][:, None] * normal[1]
        + geometry[8][:, None] * normal[2]
    )
    projected = jnp.abs(
        geometry[3][:, None] * normal[0]
        + geometry[4][:, None] * normal[1]
        + geometry[5][:, None] * normal[2]
    )
    depth_in = jnp.maximum(-gap_value, 0.0)
    weight = jnp.exp(-0.5 * dist_sq)
    return weight * depth_in * (stiff - DAMPING * closing) * projected


def local(node_data, eroded, bucket_map, seg_point, seg_angle):
    elem_count = lax.axis_size("elem")
    local_buckets = seg_point.shape[0]
    bucket_total = local_buckets * elem_count
    erode_count = eroded.shape[0]
    extract_count = 6 * erode_count
    slot_count = max(2, (10 * erode_count + bucket_total - 1) // bucket_total)
    sides = jnp.arange(6, dtype=jnp.int32)
    face_index = (6 * eroded[:, None] + sides[None, :]).reshape(extract_count)
    face_rows = jnp.take(node_data, face_index, axis=1)
    face_bucket = jnp.take(bucket_map, face_index)
    bucket_iota = jnp.arange(bucket_total, dtype=jnp.int32)

    def rank_block(carried, block_ids):
        onehot = (block_ids[:, None] == bucket_iota[None, :]).astype(jnp.int32)
        earlier = jnp.cumsum(onehot, axis=0) - onehot + carried[None, :]
        return (carried + jnp.sum(onehot, axis=0), jnp.sum(onehot * earlier, axis=1))

    local_counts, ranks = lax.scan(
        rank_block,
        jnp.zeros((bucket_total,), jnp.int32),
        face_bucket.reshape(extract_count // 128, 128),
    )
    ranks = ranks.reshape(extract_count)
    width = bucket_total * slot_count
    target = face_bucket * slot_count + ranks
    payload = face_geometry(face_rows)
    outgoing = (
        jnp.zeros((payload.shape[0], width), jnp.float32).at[:, target].set(payload, mode="drop")
    )
    incoming = lax.all_to_all(outgoing, "elem", split_axis=1, concat_axis=1, tiled=True)
    bucket_counts = lax.psum_scatter(
        local_counts.astype(jnp.float32), "elem", scatter_dimension=0, tiled=True
    )
    row_count = incoming.shape[0]
    grouped = (
        incoming.reshape(row_count, elem_count, local_buckets, slot_count)
        .transpose(2, 0, 1, 3)
        .reshape(local_buckets, row_count, elem_count * slot_count)
    )
    stiffness = STIFFNESS * lax.rsqrt(jnp.maximum(bucket_counts, 1.0))
    normals = unit_normal(seg_angle)

    def bucket_force(items):
        faces_in, points, normal, stiff = items
        traction = penalty_terms(faces_in, points[:, None, :], normal[:, None, :], stiff)
        return jnp.einsum("sg,cg->cs", traction, normal, precision=lax.Precision.HIGHEST)

    partial_force = lax.map(bucket_force, (grouped, seg_point, normals, stiffness))
    partial_force = (
        partial_force.reshape(local_buckets, 3, elem_count, slot_count)
        .transpose(1, 2, 0, 3)
        .reshape(3, width)
    )
    to_return = lax.psum(partial_force, "bucket")
    returned = lax.all_to_all(to_return, "elem", split_axis=1, concat_axis=1, tiled=True)
    picked = jnp.take(returned, target, axis=1)
    return picked


def solution(mesh):
    in_specs = (
        P(None, "elem"),
        P("elem"),
        P("elem"),
        P("elem", None, "bucket"),
        P("elem", None, "bucket"),
    )
    out_specs = P(None, "elem")
    return jax.shard_map(local, mesh=mesh, in_specs=in_specs, out_specs=out_specs, check_vma=False)
```

profile of v0, /device:TPU:0, one launch (start us, length us, event | category | flops | bytes accessed | tf_op | source)
XLA Modules:
  0.0 157.0 jit_solution(2333191016288181020)
XLA Ops:
  1.4 17.4 %gather_fusion = s32[3072]{0:T(1024)S(1)} fusion(s32[12288]{0:T(1024)S(1)} %copy-done, s32[3072]{0:T(1024)S(1)} %broadcast_clamp_fusion.1), kind=kCustom, calls=%fused_computation | custom fusion | bytes 36864 | tf_op jit(solution)/shard_map/jit(_take)/gather | solution.py:63
  18.9 12.8 %while.26 = (s32[]{:T(128)}, s32[64]{0:T(128)S(1)}, s32[24,128]{1,0:T(8,128)S(1)}, s32[24,128]{1,0:T(8,128)S(1)}) while((s32[]{:T(128)}, s32[64]{0:T(128)S(1)}, s32[24,128]{1,0:T(8,128)S(1)}, s32[24,128]{1,0:T(8,128)S(1)}) %tuple.75), condition=%wide.region_4.5_spmd.clone.clone, body=%wide.region_0.4_spmd.clone.sunk.clone | while | flops 1114115 | bytes 136524 | solution.py:71
  31.7 4.0 %copy.43 = f32[24,12288]{0,1:T(8,128)} copy(f32[24,12288]{1,0:T(8,128)S(1)} %copy-done.1) | data formatting | bytes 2359296 | tf_op args[0]
  35.6 10.9 %gather_fusion.1 = f32[3072,24]{1,0:T(8,128)S(1)} fusion(f32[24,12288]{0,1:T(8,128)} %copy.43, s32[3072]{0:T(1024)S(1)} %broadcast_clamp_fusion.1), kind=kCustom, calls=%fused_computation.1 | custom fusion | bytes 602112 | tf_op jit(solution)/shard_map/jit(_take)/gather | solution.py:62
  47.5 1.7 %copy.45 = f32[3072,9]{1,0:T(8,128)} copy(f32[3072,9]{0,1:T(8,128)S(1)} %bitcast.83) | data formatting | bytes 221184 | tf_op jit(solution)/shard_map/concatenate | solution.py:20
  49.2 9.1 %scatter_custom_fusion = f32[9,5120]{0,1:T(8,128)S(1)} fusion(s32[3072]{0:T(1024)S(1)} %bitcast.89, f32[3072,9]{1,0:T(8,128)} %copy.45, f32[]{:T(128)} %constant.70.clone.1), kind=kCustom, calls=%fused_computation.80 | custom fusion | bytes 184832 | tf_op jit(solution)/shard_map/scatter | solution.py:81
  58.3 1.5 copy.46
  59.8 7.3 %all-to-all-start = ((f32[9,8,640]{2,0,1:T(8,128)}), f32[9,8,640]{2,0,1:T(8,128)S(1)}, u32[]{:S(2)}, u32[]{:S(2)}) async-start(f32[9,8,640]{2,0,1:T(8,128)} %copy.46), calls=%async_computation | async-start | bytes 655360 | tf_op jit(solution)/shard_map/all_to_all | solution.py:83
  67.1 21.9 %all-reduce = f32[64]{0:T(128)S(1)} all-reduce(f32[64]{0:T(128)S(1)} %convert_element_type.6), channel_id=2, replica_groups=mesh['elem'=8,'bucket'=4] {'elem'}, use_global_device_ids=true, to_apply=%region_6.7.clone | all-reduce | flops 64 | bytes 512
  91.1 28.6 %while.25 = (s32[]{:T(128)}, f32[8,3,640]{2,0,1:T(8,128)S(1)}, f32[8,3,128]{2,0,1:T(8,128)S(1)}, f32[8,9,640]{2,1,0:T(8,128)S(1)}, f32[8,3,128]{2,0,1:T(8,128)}, /*index=5*/f32[8]{0:T(128)S(1)}) while((s32[]{:T(128)}, f32[8,3,640]{2,0,1:T(8,128)S(1)}, f32[8,3,128]{2,0,1:T(8,128)S(1)}, f32[8,9,640]{2,1,0:T(8,128)S(1)}, ...), condition=%wide.region_8.9_spmd.clone, body=%wide.region_7.8_spmd.sunk.clone | while | flops 5570568 | bytes 2093765 | solution.py:101
  91.1 0.7 constant_dynamic-slice_fusion.4
  92.9 1.6 %convolution_bitcast_fusion.3 = f32[1,3,640]{2,1,0:T(4,128)S(1)} fusion(f32[3,640,128]{2,1,0:T(8,128)S(1)} %broadcast_subtract_fusion.3, f32[640]{0:T(1024)S(1)} %get-tuple-element.253, f32[640]{0:T(1024)S(1)} %get-tuple-element.254, f32[640]{0:T(1024)S(1)} %get-tuple-element.255, f32[640]{0:T(1024)S(1)} %get-tuple-element.256, ...), kind=kOutput, calls=%fused_computation.12.clone.1.clone | convolution fusion | flops 5324800 | bytes 1009156 | tf_op jit(solution)/shard_map/while/body/eval_jaxpr/sg,cg->cs/dot_general | solution.py:99
  94.7 0.7 constant_dynamic-slice_fusion.4
  96.5 1.6 %convolution_bitcast_fusion.3 = f32[1,3,640]{2,1,0:T(4,128)S(1)} fusion(f32[3,640,128]{2,1,0:T(8,128)S(1)} %broadcast_subtract_fusion.3, f32[640]{0:T(1024)S(1)} %get-tuple-element.253, f32[640]{0:T(1024)S(1)} %get-tuple-element.254, f32[640]{0:T(1024)S(1)} %get-tuple-element.255, f32[640]{0:T(1024)S(1)} %get-tuple-element.256, ...), kind=kOutput, calls=%fused_computation.12.clone.1.clone | convolution fusion | flops 5324800 | bytes 1009156 | tf_op jit(solution)/shard_map/while/body/eval_jaxpr/sg,cg->cs/dot_general | solution.py:99
  98.2 0.7 constant_dynamic-slice_fusion.4
  100.0 1.6 %convolution_bitcast_fusion.3 = f32[1,3,640]{2,1,0:T(4,128)S(1)} fusion(f32[3,640,128]{2,1,0:T(8,128)S(1)} %broadcast_subtract_fusion.3, f32[640]{0:T(1024)S(1)} %get-tuple-element.253, f32[640]{0:T(1024)S(1)} %get-tuple-element.254, f32[640]{0:T(1024)S(1)} %get-tuple-element.255, f32[640]{0:T(1024)S(1)} %get-tuple-element.256, ...), kind=kOutput, calls=%fused_computation.12.clone.1.clone | convolution fusion | flops 5324800 | bytes 1009156 | tf_op jit(solution)/shard_map/while/body/eval_jaxpr/sg,cg->cs/dot_general | solution.py:99
  101.8 0.7 constant_dynamic-slice_fusion.4
  103.6 1.6 %convolution_bitcast_fusion.3 = f32[1,3,640]{2,1,0:T(4,128)S(1)} fusion(f32[3,640,128]{2,1,0:T(8,128)S(1)} %broadcast_subtract_fusion.3, f32[640]{0:T(1024)S(1)} %get-tuple-element.253, f32[640]{0:T(1024)S(1)} %get-tuple-element.254, f32[640]{0:T(1024)S(1)} %get-tuple-element.255, f32[640]{0:T(1024)S(1)} %get-tuple-element.256, ...), kind=kOutput, calls=%fused_computation.12.clone.1.clone | convolution fusion | flops 5324800 | bytes 1009156 | tf_op jit(solution)/shard_map/while/body/eval_jaxpr/sg,cg->cs/dot_general | solution.py:99
  105.4 0.7 constant_dynamic-slice_fusion.4
  107.2 1.6 %convolution_bitcast_fusion.3 = f32[1,3,640]{2,1,0:T(4,128)S(1)} fusion(f32[3,640,128]{2,1,0:T(8,128)S(1)} %broadcast_subtract_fusion.3, f32[640]{0:T(1024)S(1)} %get-tuple-element.253, f32[640]{0:T(1024)S(1)} %get-tuple-element.254, f32[640]{0:T(1024)S(1)} %get-tuple-element.255, f32[640]{0:T(1024)S(1)} %get-tuple-element.256, ...), kind=kOutput, calls=%fused_computation.12.clone.1.clone | convolution fusion | flops 5324800 | bytes 1009156 | tf_op jit(solution)/shard_map/while/body/eval_jaxpr/sg,cg->cs/dot_general | solution.py:99
  108.9 0.7 constant_dynamic-slice_fusion.4
  110.8 1.6 %convolution_bitcast_fusion.3 = f32[1,3,640]{2,1,0:T(4,128)S(1)} fusion(f32[3,640,128]{2,1,0:T(8,128)S(1)} %broadcast_subtract_fusion.3, f32[640]{0:T(1024)S(1)} %get-tuple-element.253, f32[640]{0:T(1024)S(1)} %get-tuple-element.254, f32[640]{0:T(1024)S(1)} %get-tuple-element.255, f32[640]{0:T(1024)S(1)} %get-tuple-element.256, ...), kind=kOutput, calls=%fused_computation.12.clone.1.clone | convolution fusion | flops 5324800 | bytes 1009156 | tf_op jit(solution)/shard_map/while/body/eval_jaxpr/sg,cg->cs/dot_general | solution.py:99
  112.5 0.7 constant_dynamic-slice_fusion.4
  114.3 1.6 %convolution_bitcast_fusion.3 = f32[1,3,640]{2,1,0:T(4,128)S(1)} fusion(f32[3,640,128]{2,1,0:T(8,128)S(1)} %broadcast_subtract_fusion.3, f32[640]{0:T(1024)S(1)} %get-tuple-element.253, f32[640]{0:T(1024)S(1)} %get-tuple-element.254, f32[640]{0:T(1024)S(1)} %get-tuple-element.255, f32[640]{0:T(1024)S(1)} %get-tuple-element.256, ...), kind=kOutput, calls=%fused_computation.12.clone.1.clone | convolution fusion | flops 5324800 | bytes 1009156 | tf_op jit(solution)/shard_map/while/body/eval_jaxpr/sg,cg->cs/dot_general | solution.py:99
  117.9 1.6 %convolution_bitcast_fusion.3 = f32[1,3,640]{2,1,0:T(4,128)S(1)} fusion(f32[3,640,128]{2,1,0:T(8,128)S(1)} %broadcast_subtract_fusion.3, f32[640]{0:T(1024)S(1)} %get-tuple-element.253, f32[640]{0:T(1024)S(1)} %get-tuple-element.254, f32[640]{0:T(1024)S(1)} %get-tuple-element.255, f32[640]{0:T(1024)S(1)} %get-tuple-element.256, ...), kind=kOutput, calls=%fused_computation.12.clone.1.clone | convolution fusion | flops 5324800 | bytes 1009156 | tf_op jit(solution)/shard_map/while/body/eval_jaxpr/sg,cg->cs/dot_general | solution.py:99
  119.9 10.7 %psum.7 = f32[3,8,640]{2,1,0:T(8,128)S(1)} all-reduce(f32[3,8,640]{2,1,0:T(8,128)S(1)} %all_to_all.16), channel_id=1, replica_groups=mesh['elem'=8,'bucket'=4] {'bucket'}, use_global_device_ids=true, to_apply=%region_9.10 | all-reduce | flops 15360 | bytes 122880 | tf_op jit(solution)/shard_map/psum | solution.py:107
  131.2 3.4 %all-to-all-start.1 = ((f32[3,8,640]{2,0,1:T(4,128)}), f32[3,8,640]{2,0,1:T(4,128)S(1)}, u32[]{:S(2)}, u32[]{:S(2)}) async-start(f32[3,8,640]{2,0,1:T(4,128)} %copy.54), calls=%async_computation.1 | async-start | bytes 163840 | tf_op jit(solution)/shard_map/all_to_all | solution.py:108
  134.6 6.9 %all-to-all-done.1 = f32[3,8,640]{2,0,1:T(4,128)S(1)} async-done(((f32[3,8,640]{2,0,1:T(4,128)}), f32[3,8,640]{2,0,1:T(4,128)S(1)}, u32[]{:S(2)}, u32[]{:S(2)}) %all-to-all-start.1) | async-done | bytes 61472 | tf_op jit(solution)/shard_map/all_to_all | solution.py:108
  141.5 0.8 copy.55
  142.3 10.8 %gather_fusion.2 = f32[3072,3]{1,0:T(8,128)} fusion(f32[3,5120]{0,1:T(8,128)S(1)} %bitcast.81, s32[3072]{0:T(1024)S(1)} %broadcast_clamp_fusion), kind=kCustom, calls=%fused_computation.2 | custom fusion | bytes 86016 | tf_op jit(solution)/shard_map/jit(_take)/gather | solution.py:109
  153.2 2.7 %select_bitcast_fusion = f32[3,3072]{0,1:T(8,128)S(1)} fusion(f32[3072,3]{1,0:T(8,128)} %gather_fusion.2, pred[3072]{0:T(1024)(128)(4,1)S(1)} %get-tuple-element.137), kind=kLoop, calls=%fused_computation.79 | loop fusion | flops 9216 | bytes 76800 | tf_op jit(solution)/shard_map/jit(_take)/select_n | solution.py:109
  155.9 1.1 copy.56
  (284 shorter events, 26.7 us)
Async XLA Ops:
  0.0 1.4 copy-start
  1.4 30.2 %copy-start.1 = (f32[24,12288]{1,0:T(8,128)S(1)}, f32[24,12288]{1,0:T(8,128)}, u32[]{:S(2)}) copy-start(f32[24,12288]{1,0:T(8,128)} %param.9) | copy-start | bytes 3538948
  58.3 30.8 %copy-start.2 = (f32[8,2,128]{2,1,0:T(2,128)S(1)}, f32[8,2,128]{2,1,0:T(2,128)}, u32[]{:S(2)}) copy-start(f32[8,2,128]{2,1,0:T(2,128)} %param.13) | copy-start | bytes 24580
  58.3 30.8 %copy-start.3 = (u32[32]{0:T(128)S(1)}, u32[32]{0:T(128)}, u32[]{:S(2)}) copy-start(u32[32]{0:T(128)} %constant.97) | copy-start | bytes 388
  59.8 30.8 %all-to-all-start = ((f32[9,8,640]{2,0,1:T(8,128)}), f32[9,8,640]{2,0,1:T(8,128)S(1)}, u32[]{:S(2)}, u32[]{:S(2)}) async-start(f32[9,8,640]{2,0,1:T(8,128)} %copy.46), calls=%async_computation | async-start | bytes 655360 | tf_op jit(solution)/shard_map/all_to_all | solution.py:83
  131.2 10.3 %all-to-all-start.1 = ((f32[3,8,640]{2,0,1:T(4,128)}), f32[3,8,640]{2,0,1:T(4,128)S(1)}, u32[]{:S(2)}, u32[]{:S(2)}) async-start(f32[3,8,640]{2,0,1:T(4,128)} %copy.54), calls=%async_computation.1 | async-start | bytes 163840 | tf_op jit(solution)/shard_map/all_to_all | solution.py:108
where the time goes:
time: 158 us; the launch traced here: 157 us
  local copies, waits for them, and re-layouts  74.4 us (47%)
  blocking collectives  32.6 us (21%)
  other arithmetic  17.2 us (11%)
  matrix products  12.7 us (8%)
  starting transfers between devices  10.7 us (7%)
  waiting for transfers between devices  6.94 us (4%)
    unnamed x1, blocking collectives  21.9 us
    gather x1, local copies, waits for them, and re-layouts, local(): face_bucket = jnp.take(bucket_map, face_index)  17.4 us
    dot_general x8, matrix products, bucket_force(): jnp.einsum('sg,cg->cs', traction, normal, precision=lax.Precision.HIGHEST)  12.7 us
    gather x2, local copies, waits for them, and re-layouts, local(): face_rows = jnp.take(node_data, face_index, axis=1)  11.3 us
    dynamic_slice x32, local copies, waits for them, and re-layouts, local(): lax.map(bucket_force, (grouped, seg_point, normals, stiffness))  11.2 us
    gather x1, local copies, waits for them, and re-layouts, local(): picked = jnp.take(returned, target, axis=1)  10.8 us
    psum x1, blocking collectives, local(): to_return = lax.psum(partial_force, 'bucket')  10.7 us
    scatter x1, local copies, waits for them, and re-layouts, local(): jnp.zeros((payload.shape[0], width), jnp.float32).at[:, target]  9.09 us
  transfers between devices with their start and end apart: 2, of which 1 were waited for; matrix products, arithmetic and copies ran while one was open for 1% of the time, Pallas kernels for 0%

commit v1 on v0

v1 whole, which is shorter than its diff:
```python
import functools

import jax
import jax.numpy as jnp
from jax import lax
from jax.experimental import pallas as pl
from jax.experimental.pallas import tpu as pltpu
from jax.sharding import PartitionSpec as P

STIFFNESS = 20.0
DAMPING = 0.5
LANES = 128
SIDES = 6
BLOCK = SIDES * LANES
ROWS = 32
F32 = jnp.float32
BF16 = jnp.bfloat16


def split3(x):
    hi = x.astype(BF16).astype(F32)
    rest = x - hi
    mid = rest.astype(BF16).astype(F32)
    return hi, mid, rest - mid


def sin_cos(x):
    k = jnp.floor(x * 0.6366197723675814 + 0.5)
    r = x - k * 1.5703125
    r = r - k * 4.837512969970703125e-4
    r = r - k * 7.54978995489188216e-8
    z = r * r
    s = ((-1.9515295891e-4 * z + 8.3321608736e-3) * z - 1.6666654611e-1) * z * r + r
    c = ((2.443315711809948e-5 * z - 1.388731625493765e-3) * z + 4.166664568298827e-2) * z * z
    c = c - 0.5 * z + 1.0
    q = k.astype(jnp.int32) & 3
    odd = (q & 1) == 1
    sin = jnp.where(odd, c, s)
    cos = jnp.where(odd, s, c)
    sin = jnp.where(q >= 2, -sin, sin)
    cos = jnp.where((q == 1) | (q == 2), -cos, cos)
    return sin, cos


def mm(a, b, contract=((1,), (0,))):
    return lax.dot_general(a, b, (contract, ((), ())), preferred_element_type=F32)


def kernel(
    n_elem, n_buck, node, eroded, bmap, spoint, sangle, out,
    perm, pick, rows, faces, geo, onehot, points, angles, seg_t, counts, sums_f, parts, inter,
    seg_send, seg_recv, cnt_send, cnt_recv, par_send, par_recv,
):
    me = lax.axis_index("elem")
    mb = lax.axis_index("bucket")
    own = spoint.shape[0]
    buckets = own * n_elem
    count = eroded.shape[1]
    jblocks = count // LANES
    blocks = node.shape[1] // BLOCK

    barrier = pltpu.get_barrier_semaphore()
    for d in range(1, n_elem):
        pl.semaphore_signal(
            barrier, inc=1, device_id={"elem": lax.rem(me + d, n_elem)},
            device_id_type=pl.DeviceIdType.MESH,
        )
    for d in range(1, n_buck):
        pl.semaphore_signal(
            barrier, inc=1, device_id={"bucket": lax.rem(mb + d, n_buck)},
            device_id_type=pl.DeviceIdType.MESH,
        )

    col = lax.broadcasted_iota(jnp.int32, (1, BLOCK), 1)
    source = SIDES * (col & (LANES - 1)) + (col // LANES)
    for i in range(BLOCK // 256):
        r = lax.broadcasted_iota(jnp.int32, (256, BLOCK), 0) + i * 256
        perm[i * 256:(i + 1) * 256, :] = jnp.where(r == source, 1.0, 0.0).astype(BF16)

    group = 4
    for g in range(blocks // group):
        stack = []
        for i in range(g * group, (g + 1) * group):
            lanes = slice(i * BLOCK, (i + 1) * BLOCK)
            ids = jnp.broadcast_to(bmap[:, lanes].astype(F32), (ROWS - 24, BLOCK))
            stack += [v.astype(BF16) for v in split3(jnp.concatenate([node[:, lanes], ids], axis=0))]
        apart = mm(jnp.concatenate(stack, axis=0), perm[...]).astype(BF16)
        for i in range(group):
            at = (g * group + i) * LANES
            for p in range(3):
                for s in range(SIDES):
                    top = (p * SIDES + s) * ROWS
                    r0 = (i * 3 + p) * ROWS
                    rows[top:top + ROWS, at:at + LANES] = apart[
                        r0:r0 + ROWS, s * LANES:(s + 1) * LANES
                    ]

    pl.semaphore_wait(barrier, n_elem + n_buck - 2)

    def seg_copies(slot, d, owner, target):
        at = pl.ds(owner * own, own)
        return [
            pltpu.make_async_remote_copy(
                src_ref=src, dst_ref=dst.at[at],
                send_sem=seg_send.at[i, slot], recv_sem=seg_recv.at[i, slot],
                device_id={"elem": target}, device_id_type=pl.DeviceIdType.MESH,
            )
            for i, (src, dst) in enumerate([(spoint, points), (sangle, angles)])
        ]

    for d in range(1, n_elem):
        for c in seg_copies(d - 1, d, me, lax.rem(me + d, n_elem)):
            c.start()
    points[pl.ds(me * own, own)] = spoint[...]
    angles[pl.ds(me * own, own)] = sangle[...]

    for i in range(pick.shape[0] // 256):
        r = lax.broadcasted_iota(jnp.int32, (256, count), 0) + i * 256
        pick[i * 256:(i + 1) * 256, :] = jnp.where(r == eroded[...], 1.0, 0.0).astype(BF16)
    taken = mm(rows[...], pick[...])
    third = SIDES * ROWS
    taken = (taken[0:third] + taken[third:2 * third]) + taken[2 * third:3 * third]
    for s in range(SIDES):
        faces[s] = taken[s * ROWS:(s + 1) * ROWS]

    ones = jnp.ones((8, count), BF16)
    chunk = min(buckets, LANES)
    for b in range(0, buckets, chunk):
        iota = lax.broadcasted_iota(jnp.int32, (chunk, count), 0) + b
        total = jnp.zeros((chunk, count), F32)
        for s in range(SIDES):
            ids = faces[s, 24:25, :].astype(jnp.int32)
            hot = jnp.where(iota == ids, 1.0, 0.0)
            total = total + hot
            onehot[b:b + chunk, s * count:(s + 1) * count] = hot.astype(BF16)
        if chunk < LANES:
            total = jnp.concatenate([total, jnp.zeros((LANES - chunk, count), F32)], axis=0)
        counts[me, :, b:b + LANES] = mm(ones, total.astype(BF16), ((1,), (1,)))

    def cnt_copy(slot, owner, target):
        return pltpu.make_async_remote_copy(
            src_ref=counts.at[owner], dst_ref=counts.at[owner],
            send_sem=cnt_send.at[slot], recv_sem=cnt_recv.at[slot],
            device_id={"elem": target}, device_id_type=pl.DeviceIdType.MESH,
        )

    for d in range(1, n_elem):
        cnt_copy(d - 1, me, lax.rem(me + d, n_elem)).start()

    c = [faces[:, i, :] for i in range(24)]
    e1 = [c[6 + i] - c[i] for i in range(3)]
    e2 = [c[9 + i] - c[3 + i] for i in range(3)]
    for i in range(3):
        j, k = (i + 1) % 3, (i + 2) % 3
        geo[:, i, :] = 0.25 * (c[i] + c[3 + i] + c[6 + i] + c[9 + i])
        geo[:, 3 + i, :] = 0.5 * (e1[j] * e2[k] - e1[k] * e2[j])
        geo[:, 6 + i, :] = 0.25 * (c[12 + i] + c[15 + i] + c[18 + i] + c[21 + i])

    for d in range(1, n_elem):
        for cp in seg_copies(d - 1, d, lax.rem(me + n_elem - d, n_elem), me):
            cp.wait_recv()
    chunk = min(buckets, LANES // 2)

    def lay_out(b):
        at = pl.ds(b * chunk, chunk)
        sin0, cos0 = sin_cos(angles[at, 0, :])
        sin1, cos1 = sin_cos(angles[at, 1, :])
        values = [points[at, i, :] for i in range(3)] + [cos0 * sin1, sin0 * sin1, cos1]
        for i, v in enumerate(values):
            stack = jnp.concatenate(list(split3(v)) + [jnp.zeros_like(v)], axis=0)
            lanes = pl.ds(pl.multiple_of(b * 4 * chunk, LANES), 4 * chunk)
            seg_t[i * LANES:(i + 1) * LANES, lanes] = stack.T.astype(BF16)

    if buckets == chunk:
        lay_out(0)
    else:
        pl.loop(0, buckets // chunk)(lay_out)

    half = 256
    halves = count // half

    def step(it, carry):
        s = it // halves
        h = it % halves
        hot = onehot[:, pl.ds(pl.multiple_of(it * half, half), half)]
        hot = [hot[b:b + chunk] for b in range(0, buckets, chunk) for _ in range(4)]
        sel = mm(seg_t[...], jnp.concatenate(hot, axis=0))
        for lt in range(half // LANES):
            g = geo[s, :, pl.ds(pl.multiple_of(h * half + lt * LANES, LANES), LANES)]
            g = [jnp.broadcast_to(g[i:i + 1], (8, LANES)) for i in range(9)]
            acc = [jnp.zeros((8, LANES), F32) for _ in range(6)]
            for r in range(LANES // 8):
                px, py, pz, nx, ny, nz = [
                    sel[q * LANES + r * 8:q * LANES + r * 8 + 8, lt * LANES:(lt + 1) * LANES]
                    for q in range(6)
                ]
                ox, oy, oz = g[0] - px, g[1] - py, g[2] - pz
                dist = ox * ox + oy * oy + oz * oz
                gap = ox * nx + oy * ny + oz * nz
                proj = jnp.abs(g[3] * nx + g[4] * ny + g[5] * nz)
                closing = g[6] * nx + g[7] * ny + g[8] * nz
                base = jnp.exp(-0.5 * dist) * jnp.maximum(-gap, 0.0) * proj
                damp = base * closing
                for k, n in enumerate((nx, ny, nz)):
                    acc[k] = acc[k] + base * n
                    acc[3 + k] = acc[3 + k] + damp * n
            sums = [jnp.sum(a, axis=0, keepdims=True) for a in acc]
            for k in range(6):
                sums_f[it * (half // LANES) + lt, k:k + 1, :] = sums[k]
        return carry

    lax.fori_loop(0, SIDES * halves, step, 0)

    for d in range(1, n_elem):
        cnt_copy(d - 1, lax.rem(me + n_elem - d, n_elem), me).wait_recv()
    whole = counts[0]
    for i in range(1, n_elem):
        whole = whole + counts[i]
    stiff = STIFFNESS * lax.rsqrt(jnp.maximum(whole[:, :buckets], 1.0))
    hi, mid, lo = split3(stiff)
    which = lax.broadcasted_iota(jnp.int32, stiff.shape, 0)
    stiff = jnp.where(which == 0, hi, jnp.where(which == 1, mid, jnp.where(which == 2, lo, 0.0)))
    stiff = mm(stiff.astype(BF16), onehot[...])
    stiff = (stiff[0:1] + stiff[1:2]) + stiff[2:3]
    for s in range(SIDES):
        for j in range(jblocks):
            at = s * count + j * LANES
            both = sums_f[s * jblocks + j]
            force = stiff[:, at:at + LANES] * both[0:3] - DAMPING * both[3:6]
            for k in range(3):
                parts[mb, k, j:j + 1, s * LANES:(s + 1) * LANES] = force[k:k + 1]

    def par_copy(slot, owner, target):
        return pltpu.make_async_remote_copy(
            src_ref=parts.at[owner], dst_ref=parts.at[owner],
            send_sem=par_send.at[slot], recv_sem=par_recv.at[slot],
            device_id={"bucket": target}, device_id_type=pl.DeviceIdType.MESH,
        )

    for d in range(1, n_buck):
        par_copy(d - 1, mb, lax.rem(mb + d, n_buck)).start()
    for d in range(1, n_buck):
        par_copy(d - 1, lax.rem(mb + n_buck - d, n_buck), mb).wait_recv()
    for k in range(3):
        force = parts[0, k]
        for i in range(1, n_buck):
            force = force + parts[i, k]
        for p, v in enumerate(split3(force)):
            at = (p * 3 + k) * jblocks
            inter[at:at + jblocks, :] = v
    used = 9 * jblocks
    if inter.shape[0] > used:
        inter[used:, :] = jnp.zeros((inter.shape[0] - used, BLOCK), F32)
    mixed = mm(inter[...].astype(BF16), perm[...], ((1,), (1,)))
    third = 3 * jblocks
    mixed = (mixed[0:third] + mixed[third:2 * third]) + mixed[2 * third:3 * third]
    for k in range(3):
        for j in range(jblocks):
            out[k:k + 1, j * BLOCK:(j + 1) * BLOCK] = mixed[k * jblocks + j:k * jblocks + j + 1]

    for d in range(1, n_elem):
        for cp in seg_copies(d - 1, d, me, lax.rem(me + d, n_elem)):
            cp.wait_send()
        cnt_copy(d - 1, me, lax.rem(me + d, n_elem)).wait_send()
    for d in range(1, n_buck):
        par_copy(d - 1, mb, lax.rem(mb + d, n_buck)).wait_send()


def local(n_elem, n_buck, node_data, eroded, bucket_map, seg_point, seg_angle):
    own, _, segs = seg_point.shape
    buckets = own * n_elem
    count = eroded.shape[0]
    jblocks = count // LANES
    elems = node_data.shape[1] // SIDES
    pad = -(-9 * jblocks // 16) * 16
    vmem = pl.BlockSpec(memory_space=pltpu.VMEM)
    dma = pltpu.SemaphoreType.DMA
    return pl.pallas_call(
        functools.partial(kernel, n_elem, n_buck),
        out_shape=jax.ShapeDtypeStruct((3, SIDES * count), F32),
        in_specs=[vmem] * 5,
        out_specs=vmem,
        scratch_shapes=[
            pltpu.VMEM((BLOCK, BLOCK), BF16),
            pltpu.VMEM((elems, count), BF16),
            pltpu.VMEM((3 * SIDES * ROWS, elems), BF16),
            pltpu.VMEM((SIDES, ROWS, count), F32),
            pltpu.VMEM((SIDES, 16, count), F32),
            pltpu.VMEM((buckets, SIDES * count), BF16),
            pltpu.VMEM((buckets, 3, segs), F32),
            pltpu.VMEM((buckets, 2, segs), F32),
            pltpu.VMEM((6 * segs, 4 * buckets), BF16),
            pltpu.VMEM((n_elem, 8, max(buckets, LANES)), F32),
            pltpu.VMEM((SIDES * jblocks, 8, LANES), F32),
            pltpu.VMEM((n_buck, 3, jblocks, BLOCK), F32),
            pltpu.VMEM((pad, BLOCK), F32),
            dma((2, n_elem - 1)),
            dma((2, n_elem - 1)),
            dma((n_elem - 1,)),
            dma((n_elem - 1,)),
            dma((n_buck - 1,)),
            dma((n_buck - 1,)),
        ],
        compiler_params=pltpu.CompilerParams(
            collective_id=0, has_side_effects=True, vmem_limit_bytes=60 * 1024 * 1024
        ),
        name="contact",
    )(node_data, eroded[None, :], bucket_map[None, :], seg_point, seg_angle)


def solution(mesh):
    in_specs = (
        P(None, "elem"),
        P("elem"),
        P("elem"),
        P("elem", None, "bucket"),
        P("elem", None, "bucket"),
    )
    body = functools.partial(local, mesh.shape["elem"], mesh.shape["bucket"])
    return jax.shard_map(
        body, mesh=mesh, in_specs=in_specs, out_specs=P(None, "elem"), check_vma=False
    )
```

time: 158 us -> 25.9 us (0.16)
  local copies, waits for them, and re-layouts: 74.4 us -> 2.74 us
  blocking collectives: 32.6 us -> 0 us
  Pallas kernels: 0 us -> 22.9 us
  other arithmetic: 17.2 us -> 0 us
  matrix products: 12.7 us -> 0 us
  starting transfers between devices: 10.7 us -> 0 us
  waiting for transfers between devices: 6.94 us -> 0 us
    gather x4 -> x0, local copies, waits for them, and re-layouts: 39.6 us -> none  [the longest x1 17.4 us: local(): face_bucket = jnp.take(bucket_map, face_index)]
    pallas_call x0 -> x1, Pallas kernels: none -> 22.9 us  [local(): pl.pallas_call(functools.partial(kernel, n_elem, n_buck), out_shape=jax.S...]
    unnamed x1 -> x0, blocking collectives: 21.9 us -> none
    dot_general x8 -> x0, matrix products: 12.7 us -> none  [bucket_force(): jnp.einsum('sg,cg->cs', traction, normal, precision=lax.Precision.HIGHEST)]
    dynamic_slice x32 -> x0, local copies, waits for them, and re-layouts: 11.2 us -> none  [local(): lax.map(bucket_force, (grouped, seg_point, normals, stiffness))]
    psum x1 -> x0, blocking collectives: 10.7 us -> none  [local(): to_return = lax.psum(partial_force, 'bucket')]
    all_to_all x2 -> x0, starting transfers between devices: 10.7 us -> none  [the longest x1 7.31 us: local(): lax.all_to_all(outgoing, 'elem', split_axis=1, concat_axis=1, tiled=True)]
    scatter x1 -> x0, local copies, waits for them, and re-layouts: 9.09 us -> none  [local(): jnp.zeros((payload.shape[0], width), jnp.float32).at[:, target]]
  transfers between devices with their start and end apart: 2 -> 0, of which waited for: 1 -> 0; matrix products, arithmetic and copies ran while one was open for 1% -> 0% of each run, Pallas kernels for 0% -> 0%
where the time goes in v1:
time: 25.9 us; the launch traced here: 25.7 us
  Pallas kernels  22.9 us (88%)
  local copies, waits for them, and re-layouts  2.74 us (11%)
    pallas_call x1, Pallas kernels, local(): pl.pallas_call(functools.partial(kernel, n_elem, n_buck), out_shape=jax.S...  22.9 us
    unnamed x2, local copies, waits for them, and re-layouts  2.74 us

profile of v1, /device:TPU:0, one launch (start us, length us, event | category | flops | bytes accessed | tf_op | source)
XLA Modules:
  0.0 25.7 jit_solution(6437185636805875195)
XLA Ops:
  0.0 1.3 %copy.6.spoint = f32[8,3,128]{2,1,0:T(4,128)} copy(f32[8,3,128]{2,0,1:T(8,128)} %param.8) | data formatting | bytes 24576 | tf_op args[3]
  1.3 22.9 %contact.1 = f32[3,3072]{1,0:T(4,128)} custom-call(f32[24,12288]{1,0:T(8,128)} %node.1, s32[1,512]{1,0:T(1,128)} %bitcast.3, s32[1,12288]{1,0:T(1,128)} %bitcast.2, f32[8,3,128]{2,1,0:T(4,128)} %copy.6.spoint, f32[8,2,128]{2,1,0:T(2,128)} %sangle.1), custom_call_target="tpu_custom_call" | custom-call | tf_op jit(solution)/shard_map/contact/pallas_call | solution.py:278
  24.2 1.4 %copy.8 = f32[3,3072]{1,0:T(4,128)} copy(f32[3,3072]{1,0:T(4,128)} %contact.1) | data formatting | bytes 73728

commit v2 on v1

v2 whole, which is shorter than its diff:
```python
import functools

import jax
import jax.numpy as jnp
from jax import lax
from jax.experimental import pallas as pl
from jax.experimental.pallas import tpu as pltpu
from jax.sharding import PartitionSpec as P

STIFFNESS = 20.0
DAMPING = 0.5
LANES = 128
SIDES = 6
BLOCK = SIDES * LANES
F32 = jnp.float32
BF16 = jnp.bfloat16


def split3(x):
    hi = x.astype(BF16).astype(F32)
    rest = x - hi
    mid = rest.astype(BF16).astype(F32)
    return hi, mid, rest - mid


def sin_cos(x):
    k = jnp.floor(x * 0.6366197723675814 + 0.5)
    r = x - k * 1.5703125
    r = r - k * 4.837512969970703125e-4
    r = r - k * 7.54978995489188216e-8
    z = r * r
    s = ((-1.9515295891e-4 * z + 8.3321608736e-3) * z - 1.6666654611e-1) * z * r + r
    c = ((2.443315711809948e-5 * z - 1.388731625493765e-3) * z + 4.166664568298827e-2) * z * z
    c = c - 0.5 * z + 1.0
    q = k.astype(jnp.int32) & 3
    odd = (q & 1) == 1
    sin = jnp.where(odd, c, s)
    cos = jnp.where(odd, s, c)
    sin = jnp.where(q >= 2, -sin, sin)
    cos = jnp.where((q == 1) | (q == 2), -cos, cos)
    return sin, cos


def mm(a, b, contract=((1,), (0,))):
    return lax.dot_general(a, b, (contract, ((), ())), preferred_element_type=F32)


def kernel(
    n_elem, n_buck, node_any, eroded, bmap, spoint, sangle, out,
    node, perm, pick, rows, faces, onehot, points, angles, values, seg_t, counts,
    sel0, sel1, sums_f, parts, inter,
    node_sem, seg_send, seg_recv, cnt_send, cnt_recv, par_send, par_recv,
):
    me = lax.axis_index("elem")
    mb = lax.axis_index("bucket")
    own = sangle.shape[0]
    buckets = own * n_elem
    count = eroded.shape[1]
    jblocks = count // LANES
    blocks = node.shape[1] // BLOCK
    chunks = parts.shape[1]
    mesh_ids = pl.DeviceIdType.MESH

    barrier = pltpu.get_barrier_semaphore()
    for d in range(1, n_elem):
        to = {"elem": lax.rem(me + d, n_elem)}
        pl.semaphore_signal(barrier, inc=1, device_id=to, device_id_type=mesh_ids)
    for d in range(1, n_buck):
        to = {"bucket": lax.rem(mb + d, n_buck)}
        pl.semaphore_signal(barrier, inc=1, device_id=to, device_id_type=mesh_ids)
    fetch = pltpu.make_async_copy(node_any, node, node_sem)
    fetch.start()

    col = lax.broadcasted_iota(jnp.int32, (1, BLOCK), 1)
    source = SIDES * (col & (LANES - 1)) + (col // LANES)
    for i in range(BLOCK // 256):
        r = lax.broadcasted_iota(jnp.int32, (256, BLOCK), 0) + i * 256
        perm[i * 256:(i + 1) * 256, :] = jnp.where(r == source, 1.0, 0.0).astype(BF16)
    for i in range(pick.shape[0] // 256):
        r = lax.broadcasted_iota(jnp.int32, (256, count), 0) + i * 256
        pick[i * 256:(i + 1) * 256, :] = jnp.where(r == eroded[...], 1.0, 0.0).astype(BF16)

    pl.semaphore_wait(barrier, n_elem + n_buck - 2)

    def seg_copies(slot, owner, target):
        at = pl.ds(pl.multiple_of(owner * own, own), own)
        return [
            pltpu.make_async_remote_copy(
                src_ref=src, dst_ref=dst,
                send_sem=seg_send.at[i, slot], recv_sem=seg_recv.at[i, slot],
                device_id={"elem": target}, device_id_type=mesh_ids,
            )
            for i, (src, dst) in enumerate(
                [(spoint, points.at[:, at]), (sangle, angles.at[at])]
            )
        ]

    for d in range(1, n_elem):
        for c in seg_copies(d - 1, me, lax.rem(me + d, n_elem)):
            c.start()

    fetch.wait()
    group = 4
    for g in range(blocks // group):
        stack = []
        for i in range(g * group, (g + 1) * group):
            lanes = slice(i * BLOCK, (i + 1) * BLOCK)
            c = [node[3 * v:3 * v + 3, lanes] for v in range(8)]
            e1, e2 = c[2] - c[0], c[3] - c[1]
            r1 = jnp.concatenate([e1[1:3], e1[0:1]], axis=0)
            r2 = jnp.concatenate([e2[1:3], e2[0:1]], axis=0)
            area = 0.5 * (e1 * r2 - r1 * e2)
            centroid = 0.25 * (((c[0] + c[1]) + c[2]) + c[3])
            velocity = 0.25 * (((c[4] + c[5]) + c[6]) + c[7])
            ids = bmap[:, lanes].astype(F32)
            two = jnp.zeros((2, BLOCK), F32)
            four = jnp.zeros((4, BLOCK), F32)
            first = jnp.concatenate([centroid, area, two], axis=0)
            second = jnp.concatenate([velocity, ids, four], axis=0)
            a, b = split3(first), split3(second)
            stack += [a[0], b[0], a[1], b[1], a[2]]
        apart = mm(jnp.concatenate(stack, axis=0).astype(BF16), perm[...]).astype(BF16)
        for i in range(group):
            at = (g * group + i) * LANES
            for s in range(SIDES):
                rows[s * 40:(s + 1) * 40, at:at + LANES] = apart[
                    i * 40:(i + 1) * 40, s * LANES:(s + 1) * LANES
                ]

    taken = mm(rows[...], pick[...])
    for s in range(SIDES):
        t = [taken[s * 40 + i * 8:s * 40 + i * 8 + 8] for i in range(5)]
        faces[s, 0:8, :] = (t[0] + t[2]) + t[4]
        faces[s, 8:16, :] = t[1] + t[3]

    ones = jnp.ones((8, count), BF16)
    chunk = min(buckets, LANES)
    for b in range(0, buckets, chunk):
        iota = lax.broadcasted_iota(jnp.int32, (chunk, count), 0) + b
        total = jnp.zeros((chunk, count), F32)
        for s in range(SIDES):
            ids = faces[s, 11:12, :].astype(jnp.int32)
            hot = jnp.where(iota == ids, 1.0, 0.0)
            total = total + hot
            onehot[b:b + chunk, s * count:(s + 1) * count] = hot.astype(BF16)
        if chunk < LANES:
            total = jnp.concatenate([total, jnp.zeros((LANES - chunk, count), F32)], axis=0)
        counts[me, :, b:b + LANES] = mm(ones, total.astype(BF16), ((1,), (1,)))

    def cnt_copy(slot, owner, target):
        return pltpu.make_async_remote_copy(
            src_ref=counts.at[owner], dst_ref=counts.at[owner],
            send_sem=cnt_send.at[slot], recv_sem=cnt_recv.at[slot],
            device_id={"elem": target}, device_id_type=mesh_ids,
        )

    for d in range(1, n_elem):
        cnt_copy(d - 1, me, lax.rem(me + d, n_elem)).start()

    def unfold(owner, p, a):
        at = pl.ds(pl.multiple_of(owner * own, own), own)
        sin0, cos0 = sin_cos(a[:, 0, :])
        sin1, cos1 = sin_cos(a[:, 1, :])
        for i, v in enumerate([p[0], p[1], p[2], cos0 * sin1, sin0 * sin1, cos1]):
            values[i, at, :] = v

    unfold(me, spoint[...], sangle[...])
    order = sorted(range(1, n_elem), key=lambda d: min(d, n_elem - d))
    for d in order:
        owner = lax.rem(me + n_elem - d, n_elem)
        for cp in seg_copies(d - 1, owner, me):
            cp.wait_recv()
        at = pl.ds(pl.multiple_of(owner * own, own), own)
        unfold(owner, points[:, at, :], angles[at])

    chunk = min(buckets, LANES // 2)

    def lay_out(b):
        for i in range(6):
            v = values[i, pl.ds(pl.multiple_of(b * chunk, chunk), chunk), :]
            stack = jnp.concatenate(list(split3(v)) + [jnp.zeros_like(v)], axis=0)
            lanes = pl.ds(pl.multiple_of(b * 4 * chunk, LANES), 4 * chunk)
            seg_t[i * LANES:(i + 1) * LANES, lanes] = stack.T.astype(BF16)

    if buckets == chunk:
        lay_out(0)
    else:
        pl.loop(0, buckets // chunk)(lay_out)

    for d in range(1, n_elem):
        cnt_copy(d - 1, lax.rem(me + n_elem - d, n_elem), me).wait_recv()
    whole = counts[0]
    for i in range(1, n_elem):
        whole = whole + counts[i]
    stiff = STIFFNESS * lax.rsqrt(jnp.maximum(whole[:, :buckets], 1.0))
    hi, mid, lo = split3(stiff)
    which = lax.broadcasted_iota(jnp.int32, stiff.shape, 0)
    stiff = jnp.where(which == 0, hi, jnp.where(which == 1, mid, jnp.where(which == 2, lo, 0.0)))
    stiff = mm(stiff.astype(BF16), onehot[...])
    stiff = (stiff[0:1] + stiff[1:2]) + stiff[2:3]
    for s in range(SIDES):
        faces[s, 12:13, :] = stiff[:, s * count:(s + 1) * count]

    half = 256
    halves = count // half
    steps = SIDES * halves

    def select(it, sel):
        hot = onehot[:, pl.ds(pl.multiple_of(it * half, half), half)]
        hot = [hot[b:b + chunk] for b in range(0, buckets, chunk) for _ in range(4)]
        sel[...] = mm(seg_t[...], jnp.concatenate(hot, axis=0))

    def forces(it, sel):
        s = it // halves
        h = it % halves
        for lt in range(half // LANES):
            g = faces[s, :, pl.ds(pl.multiple_of(h * half + lt * LANES, LANES), LANES)]
            cx, cy, cz, az, ax, ay, _, _, vx, vy, vz, _, stf = [
                jnp.broadcast_to(g[i:i + 1], (8, LANES)) for i in range(13)
            ]
            vx, vy, vz = DAMPING * vx, DAMPING * vy, DAMPING * vz
            acc = [jnp.zeros((8, LANES), F32) for _ in range(3)]
            for r in range(LANES // 8):
                px, py, pz, nx, ny, nz = [
                    sel[q * LANES + r * 8:q * LANES + r * 8 + 8, lt * LANES:(lt + 1) * LANES]
                    for q in range(6)
                ]
                ox, oy, oz = px - cx, py - cy, pz - cz
                dist = ox * ox + oy * oy + oz * oz
                depth = jnp.maximum(ox * nx + oy * ny + oz * nz, 0.0)
                proj = jnp.abs(ax * nx + ay * ny + az * nz)
                push = stf - (vx * nx + vy * ny + vz * nz)
                traction = (jnp.exp(-0.5 * dist) * depth) * (push * proj)
                for k, n in enumerate((nx, ny, nz)):
                    acc[k] = acc[k] + traction * n
            for k in range(3):
                at = it * (half // LANES) + lt
                sums_f[at, k:k + 1, :] = jnp.sum(acc[k], axis=0, keepdims=True)

    def par_copy(c, slot, owner, target):
        return pltpu.make_async_remote_copy(
            src_ref=parts.at[owner, c], dst_ref=parts.at[owner, c],
            send_sem=par_send.at[c, slot], recv_sem=par_recv.at[c, slot],
            device_id={"bucket": target}, device_id_type=mesh_ids,
        )

    wide = SIDES // chunks
    select(0, sel0)
    for c in range(chunks):
        base = c * steps // chunks

        def step(i, carry):
            it = base + 2 * i
            select(it + 1, sel1)
            forces(it, sel0)
            select(lax.rem(it + 2, steps), sel0)
            forces(it + 1, sel1)
            return carry

        lax.fori_loop(0, steps // chunks // 2, step, 0)
        for s in range(wide):
            for j in range(jblocks):
                f = sums_f[(c * wide + s) * jblocks + j]
                for k in range(3):
                    parts[mb, c, k, j:j + 1, s * LANES:(s + 1) * LANES] = f[k:k + 1]
        for d in range(1, n_buck):
            par_copy(c, d - 1, mb, lax.rem(mb + d, n_buck)).start()

    for c in range(chunks):
        for d in range(1, n_buck):
            par_copy(c, d - 1, lax.rem(mb + n_buck - d, n_buck), mb).wait_recv()
        for k in range(3):
            force = parts[0, c, k]
            for i in range(1, n_buck):
                force = force + parts[i, c, k]
            for p, v in enumerate(split3(force)):
                at = (p * 3 + k) * jblocks
                inter[at:at + jblocks, c * wide * LANES:(c + 1) * wide * LANES] = v
    used = 9 * jblocks
    if inter.shape[0] > used:
        inter[used:, :] = jnp.zeros((inter.shape[0] - used, BLOCK), F32)
    mixed = mm(inter[...].astype(BF16), perm[...], ((1,), (1,)))
    third = 3 * jblocks
    mixed = (mixed[0:third] + mixed[third:2 * third]) + mixed[2 * third:3 * third]
    for k in range(3):
        for j in range(jblocks):
            out[k:k + 1, j * BLOCK:(j + 1) * BLOCK] = mixed[k * jblocks + j:k * jblocks + j + 1]

    for d in range(1, n_elem):
        for cp in seg_copies(d - 1, me, lax.rem(me + d, n_elem)):
            cp.wait_send()
        cnt_copy(d - 1, me, lax.rem(me + d, n_elem)).wait_send()
    for c in range(chunks):
        for d in range(1, n_buck):
            par_copy(c, d - 1, mb, lax.rem(mb + d, n_buck)).wait_send()


def local(n_elem, n_buck, node_data, eroded, bucket_map, seg_point, seg_angle):
    own, _, segs = seg_point.shape
    buckets = own * n_elem
    count = eroded.shape[0]
    jblocks = count // LANES
    elems = node_data.shape[1] // SIDES
    pad = -(-9 * jblocks // 16) * 16
    vmem = pl.BlockSpec(memory_space=pltpu.VMEM)
    dma = pltpu.SemaphoreType.DMA
    return pl.pallas_call(
        functools.partial(kernel, n_elem, n_buck),
        out_shape=jax.ShapeDtypeStruct((3, SIDES * count), F32),
        in_specs=[pl.BlockSpec(memory_space=pl.ANY)] + [vmem] * 4,
        out_specs=vmem,
        scratch_shapes=[
            pltpu.VMEM(node_data.shape, F32),
            pltpu.VMEM((BLOCK, BLOCK), BF16),
            pltpu.VMEM((elems, count), BF16),
            pltpu.VMEM((SIDES * 40, elems), BF16),
            pltpu.VMEM((SIDES, 16, count), F32),
            pltpu.VMEM((buckets, SIDES * count), BF16),
            pltpu.VMEM((3, buckets, segs), F32),
            pltpu.VMEM((buckets, 2, segs), F32),
            pltpu.VMEM((6, buckets, segs), F32),
            pltpu.VMEM((6 * segs, 4 * buckets), BF16),
            pltpu.VMEM((n_elem, 8, max(buckets, LANES)), F32),
            pltpu.VMEM((6 * segs, 256), F32),
            pltpu.VMEM((6 * segs, 256), F32),
            pltpu.VMEM((SIDES * jblocks, 8, LANES), F32),
            pltpu.VMEM((n_buck, 3, 3, jblocks, BLOCK // 3), F32),
            pltpu.VMEM((pad, BLOCK), F32),
            dma,
            dma((2, n_elem - 1)),
            dma((2, n_elem - 1)),
            dma((n_elem - 1,)),
            dma((n_elem - 1,)),
            dma((3, n_buck - 1)),
            dma((3, n_buck - 1)),
        ],
        compiler_params=pltpu.CompilerParams(
            collective_id=0, has_side_effects=True, vmem_limit_bytes=60 * 1024 * 1024
        ),
        name="contact",
    )(node_data, eroded[None, :], bucket_map[None, :], seg_point.transpose(1, 0, 2), seg_angle)


def solution(mesh):
    in_specs = (
        P(None, "elem"),
        P("elem"),
        P("elem"),
        P("elem", None, "bucket"),
        P("elem", None, "bucket"),
    )
    body = functools.partial(local, mesh.shape["elem"], mesh.shape["bucket"])
    return jax.shard_map(
        body, mesh=mesh, in_specs=in_specs, out_specs=P(None, "elem"), check_vma=False
    )
```

time: 25.9 us -> 21.9 us (0.85)
  Pallas kernels: 22.9 us -> 20.2 us
  local copies, waits for them, and re-layouts: 2.74 us -> 1.43 us
    pallas_call x1, Pallas kernels: 22.9 us -> 20.2 us  [local(): pl.pallas_call(functools.partial(kernel, n_elem, n_buck), out_shape=jax.S...]
    unnamed x2 -> x1, local copies, waits for them, and re-layouts: 2.74 us -> 1.43 us
where the time goes in v2:
time: 21.9 us; the launch traced here: 21.7 us
  Pallas kernels  20.2 us (92%)
  local copies, waits for them, and re-layouts  1.43 us (7%)
    pallas_call x1, Pallas kernels, local(): pl.pallas_call(functools.partial(kernel, n_elem, n_buck), out_shape=jax.S...  20.2 us
    unnamed x1, local copies, waits for them, and re-layouts  1.43 us

profile of v2, /device:TPU:0, one launch (start us, length us, event | category | flops | bytes accessed | tf_op | source)
XLA Modules:
  0.0 21.7 jit_solution(7666908230957560125)
XLA Ops:
  0.0 20.2 %contact.1 = f32[3,3072]{1,0:T(4,128)} custom-call(f32[24,12288]{1,0:T(8,128)} %node_any.1, s32[1,512]{1,0:T(1,128)} %bitcast.5, s32[1,12288]{1,0:T(1,128)} %bitcast.3, f32[3,8,128]{2,1,0:T(8,128)} %bitcast.4, f32[8,2,128]{2,1,0:T(2,128)} %sangle.1), custom_call_target="tpu_custom_call" | custom-call | tf_op jit(solution)/shard_map/contact/pallas_call | solution.py:307
  20.2 1.4 %copy.7 = f32[3,3072]{1,0:T(4,128)} copy(f32[3,3072]{1,0:T(4,128)} %contact.1) | data formatting | bytes 73728

commit v3 on v2

--- a/solution.py
+++ b/solution.py
@@ -9,6 +9,7 @@
 
 STIFFNESS = 20.0
 DAMPING = 0.5
+HALF_LOG2E = -0.7213475204444817
 LANES = 128
 SIDES = 6
 BLOCK = SIDES * LANES
@@ -80,8 +81,6 @@
         r = lax.broadcasted_iota(jnp.int32, (256, count), 0) + i * 256
         pick[i * 256:(i + 1) * 256, :] = jnp.where(r == eroded[...], 1.0, 0.0).astype(BF16)
 
-    pl.semaphore_wait(barrier, n_elem + n_buck - 2)
-
     def seg_copies(slot, owner, target):
         at = pl.ds(pl.multiple_of(owner * own, own), own)
         return [
@@ -95,13 +94,15 @@
             )
         ]
 
-    for d in range(1, n_elem):
-        for c in seg_copies(d - 1, me, lax.rem(me + d, n_elem)):
-            c.start()
-
     fetch.wait()
     group = 4
+    order = sorted(range(1, n_elem), key=lambda d: min(d, n_elem - d))
     for g in range(blocks // group):
+        if g == blocks // group // 2:
+            pl.semaphore_wait(barrier, n_elem + n_buck - 2)
+            for d in reversed(order):
+                for cp in seg_copies(d - 1, me, lax.rem(me + d, n_elem)):
+                    cp.start()
         stack = []
         for i in range(g * group, (g + 1) * group):
             lanes = slice(i * BLOCK, (i + 1) * BLOCK)
@@ -145,7 +146,7 @@
             onehot[b:b + chunk, s * count:(s + 1) * count] = hot.astype(BF16)
         if chunk < LANES:
             total = jnp.concatenate([total, jnp.zeros((LANES - chunk, count), F32)], axis=0)
-        counts[me, :, b:b + LANES] = mm(ones, total.astype(BF16), ((1,), (1,)))
+        counts[me, :, b:b + LANES] = mm(ones, total.astype(BF16), ((1,), (1,)))[0:1]
 
     def cnt_copy(slot, owner, target):
         return pltpu.make_async_remote_copy(
@@ -165,7 +166,6 @@
             values[i, at, :] = v
 
     unfold(me, spoint[...], sangle[...])
-    order = sorted(range(1, n_elem), key=lambda d: min(d, n_elem - d))
     for d in order:
         owner = lax.rem(me + n_elem - d, n_elem)
         for cp in seg_copies(d - 1, owner, me):
@@ -192,7 +192,8 @@
     whole = counts[0]
     for i in range(1, n_elem):
         whole = whole + counts[i]
-    stiff = STIFFNESS * lax.rsqrt(jnp.maximum(whole[:, :buckets], 1.0))
+    whole = jnp.broadcast_to(whole[:, :buckets], (8, buckets))
+    stiff = STIFFNESS * lax.rsqrt(jnp.maximum(whole, 1.0))
     hi, mid, lo = split3(stiff)
     which = lax.broadcasted_iota(jnp.int32, stiff.shape, 0)
     stiff = jnp.where(which == 0, hi, jnp.where(which == 1, mid, jnp.where(which == 2, lo, 0.0)))
@@ -230,7 +231,7 @@
                 depth = jnp.maximum(ox * nx + oy * ny + oz * nz, 0.0)
                 proj = jnp.abs(ax * nx + ay * ny + az * nz)
                 push = stf - (vx * nx + vy * ny + vz * nz)
-                traction = (jnp.exp(-0.5 * dist) * depth) * (push * proj)
+                traction = (jnp.exp2(HALF_LOG2E * dist) * depth) * (push * proj)
                 for k, n in enumerate((nx, ny, nz)):
                     acc[k] = acc[k] + traction * n
             for k in range(3):
@@ -320,7 +321,7 @@
             pltpu.VMEM((buckets, 2, segs), F32),
             pltpu.VMEM((6, buckets, segs), F32),
             pltpu.VMEM((6 * segs, 4 * buckets), BF16),
-            pltpu.VMEM((n_elem, 8, max(buckets, LANES)), F32),
+            pltpu.VMEM((n_elem, 1, max(buckets, LANES)), F32),
             pltpu.VMEM((6 * segs, 256), F32),
             pltpu.VMEM((6 * segs, 256), F32),
             pltpu.VMEM((SIDES * jblocks, 8, LANES), F32),

time: 21.9 us -> 22.8 us (1.041)
  Pallas kernels: 20.2 us -> 21.1 us
    pallas_call x1, Pallas kernels: 20.2 us -> 21.1 us  [local(): pl.pallas_call(functools.partial(kernel, n_elem, n_buck), out_shape=jax.S...]
where the time goes in v3:
time: 22.8 us; the launch traced here: 22.6 us
  Pallas kernels  21.1 us (93%)
  local copies, waits for them, and re-layouts  1.43 us (6%)
    pallas_call x1, Pallas kernels, local(): pl.pallas_call(functools.partial(kernel, n_elem, n_buck), out_shape=jax.S...  21.1 us
    unnamed x1, local copies, waits for them, and re-layouts  1.43 us

profile of v3, /device:TPU:0, one launch (start us, length us, event | category | flops | bytes accessed | tf_op | source)
XLA Modules:
  0.0 22.6 jit_solution(7982156183186478396)
XLA Ops:
  0.0 21.1 %contact.1 = f32[3,3072]{1,0:T(4,128)} custom-call(f32[24,12288]{1,0:T(8,128)} %node_any.1, s32[1,512]{1,0:T(1,128)} %bitcast.5, s32[1,12288]{1,0:T(1,128)} %bitcast.3, f32[3,8,128]{2,1,0:T(8,128)} %bitcast.4, f32[8,2,128]{2,1,0:T(2,128)} %sangle.1), custom_call_target="tpu_custom_call" | custom-call | tf_op jit(solution)/shard_map/contact/pallas_call | solution.py:308
  21.2 1.4 %copy.7 = f32[3,3072]{1,0:T(4,128)} copy(f32[3,3072]{1,0:T(4,128)} %contact.1) | data formatting | bytes 73728
